TPU v7x, 32 devices: a whole 2x2x4 slice. The times are simulated.
32 devices in a mesh: client: 8 (over z, x), head: 4 (over y, core).
Axes of the slice: x: 2, y: 2, z: 4, core: 2. Of those that a mesh axis runs over, the one named last changes fastest.
Arguments:
- pre: bfloat16 [10240, 4096], P('client'), may hold values from -40 to 40
- delta: float32 [10240, 4096], P('client', 'head'), may hold values from -300 to 300
- head_weight: bfloat16 [4096, 4096], P(None, 'head'), may hold values from -0.09375 to 0.09375
- client_ids: int32 [128], P('client'), may hold values from 0 to 127, as said below
Outputs:
- head_grad: float32 [4096, 4096], P('client', 'head')
- bias_grad: float32 [4096], P('head')
- embed_grad: float32 [128, 4096], P('client', 'head')
- span_grad: float32 [80, 4096], P(None, 'head')
Inputs may be any that keep to these rules, and one draw needn't show every extreme that they name: `client_ids`: each of the 128 clients appears exactly once.
All inputs are finite; a program needn't handle non-finite values.
Results may differ from a plain program's by a relative error of at most 0.024.
Values may be sent and summed in bfloat16 or wider, within the bound.
A program may use at most 128 MiB of HBM per device.

v0:
```python
import jax
import jax.numpy as jnp
from jax import lax
from jax.sharding import PartitionSpec as P

EPSILON = 1e-06


def silu_slope(values):
    sigma = jax.nn.sigmoid(values)
    return sigma * (1.0 + values * (1.0 - sigma))


def clip_factor(total, number):
    return jnp.minimum(1.0, 1.0 / jnp.sqrt(total / number + EPSILON))


def per_device(pre, delta, head_weight, client_ids):
    rows_here, hidden_width = pre.shape
    emit_here = delta.shape[1]
    clients_here = client_ids.shape[0]
    span_count = rows_here // clients_here
    head_devices = lax.axis_size("head")
    client_devices = lax.axis_size("client")
    hidden = jax.nn.silu(pre.astype(jnp.float32)).astype(jnp.bfloat16)
    delta_low = delta.astype(jnp.bfloat16)
    head_raw = lax.psum_scatter(
        lax.dot_general(
            hidden, delta_low, (((0,), (0,)), ((), ())), preferred_element_type=jnp.float32
        ).astype(jnp.bfloat16),
        "client",
        scatter_dimension=0,
        tiled=True,
    ).astype(jnp.float32)
    head_square = jnp.sum(head_raw * head_raw)
    head_square = lax.psum(head_square, ("client", "head"))
    bias_local = jnp.sum(delta, axis=0)
    partial_sum = lax.dot_general(
        delta_low, head_weight, (((1,), (1,)), ((), ())), preferred_element_type=jnp.float32
    )
    rounded = lax.optimization_barrier(partial_sum.astype(jnp.bfloat16))
    block_grad = rounded.astype(jnp.float32) * silu_slope(pre.astype(jnp.float32))
    grouped = block_grad.reshape(clients_here, span_count, hidden_width)
    client_whole = jnp.sum(grouped, axis=1)
    span_whole = jnp.sum(grouped, axis=0)
    client_part, span_part = (
        lax.psum_scatter(
            client_whole.astype(jnp.bfloat16), "head", scatter_dimension=1, tiled=True
        ).astype(jnp.float32),
        lax.psum_scatter(
            span_whole.astype(jnp.bfloat16), "head", scatter_dimension=1, tiled=True
        ).astype(jnp.float32),
    )
    span_raw, bias_raw = (
        lax.psum(span_part.astype(jnp.bfloat16), "client").astype(jnp.float32),
        lax.psum(bias_local.astype(jnp.bfloat16), "client").astype(jnp.float32),
    )
    targets = lax.iota(jnp.int32, lax.axis_size("client") * clients_here)
    selector = (targets[:, None] == client_ids[None, :]).astype(jnp.float32)
    embed_raw = lax.psum_scatter(
        jnp.dot(
            selector,
            client_part,
            precision=lax.Precision.HIGHEST,
            preferred_element_type=jnp.float32,
        ).astype(jnp.bfloat16),
        "client",
        scatter_dimension=0,
        tiled=True,
    ).astype(jnp.float32)
    leading = (lax.axis_index("client") == 0).astype(jnp.float32)
    small_square = leading * (jnp.sum(span_raw * span_raw) + jnp.sum(bias_raw * bias_raw))
    embed_square = jnp.sum(embed_raw * embed_raw)
    embed_total, small_total = lax.psum((embed_square, small_square), ("client", "head"))
    emit_total = emit_here * head_devices
    clients_total = clients_here * client_devices
    head_factor = clip_factor(head_square, hidden_width * emit_total)
    embed_factor = clip_factor(embed_total, clients_total * hidden_width)
    rest_factor = clip_factor(small_total, span_count * hidden_width + emit_total)
    return (
        head_factor * head_raw,
        rest_factor * bias_raw,
        embed_factor * embed_raw,
        rest_factor * span_raw,
    )


def solution(mesh):
    placed = (P("client", None), P("client", "head"), P(None, "head"), P("client"))
    return jax.shard_map(
        per_device,
        mesh=mesh,
        in_specs=placed,
        out_specs=(P("client", "head"), P("head"), P("client", "head"), P(None, "head")),
        check_vma=False,
    )
```

profile of v0, /device:TPU:0, one launch (start us, length us, event | category | flops | bytes accessed | tf_op | source)
XLA Modules:
  0.0 433.6 jit_solution(12990887152646815512)
XLA Ops:
  7.2 17.6 %convolution_convert_fusion = bf16[1280,4096]{1,0:T(8,128)(2,1)} fusion(bf16[4096,1024]{1,0:T(8,128)(2,1)} %param.6, f32[1280,1024]{1,0:T(8,128)} %param.5), kind=kOutput, calls=%fused_computation.10 | convolution fusion | flops 10743971840 | bytes 24117248 | tf_op jit(solution)/shard_map/dot_general | solution.py:38
  24.8 9.6 %fusion.6 = f32[1280,4096]{1,0:T(8,128)S(1)} fusion(bf16[1280,4096]{1,0:T(8,128)(2,1)S(1)} %copy-done, bf16[1280,4096]{1,0:T(8,128)(2,1)} %convolution_convert_fusion), kind=kLoop, calls=%fused_computation.9 | loop fusion | flops 52428800 | bytes 41943040 | tf_op jit(solution)/shard_map/mul | solution.py:42
  34.4 5.2 %fusion.20 = (bf16[16,4096]{1,0:T(8,128)(2,1)}, bf16[80,4096]{1,0:T(8,128)(2,1)}) fusion(f32[16,80,4096]{2,1,0:T(8,128)S(1)} %bitcast.3), kind=kLoop, calls=%fused_computation.31 | loop fusion | flops 10092544 | bytes 21757952 | tf_op jit(solution)/shard_map/reduce_sum | solution.py:44
  39.6 0.0 reduce-scatter.7.cloned.1.call-start
  39.6 0.7 reduce-scatter.7.cloned.1.call-update
  40.4 21.7 %reduce-scatter.9.cloned.1.call-done = bf16[16,1024]{1,0:T(8,128)(2,1)} async-done(((bf16[16,4096]{1,0:T(8,128)(2,1)}), bf16[16,1024]{1,0:T(8,128)(2,1)}) %reduce-scatter.9.cloned.1.call-update) | async-done | bytes 32784 | tf_op jit(solution)/shard_map/reduce_scatter | solution.py:47
  62.1 1.7 convolution_convert_fusion.1
  63.8 23.8 %reduce-scatter.7.cloned.1.call-done = bf16[80,1024]{1,0:T(8,128)(2,1)} async-done(((bf16[80,4096]{1,0:T(8,128)(2,1)}), bf16[80,1024]{1,0:T(8,128)(2,1)}) %reduce-scatter.7.cloned.1.call-update) | async-done | bytes 163856 | tf_op jit(solution)/shard_map/reduce_scatter | solution.py:50
  87.6 0.2 reduce-scatter.5.cloned.1.call-start
  87.9 18.3 %fusion.9 = bf16[4096,1024]{1,0:T(8,128)(2,1)} fusion(bf16[1280,4096]{1,0:T(8,128)(2,1)} %param.4, f32[1280,1024]{1,0:T(8,128)} %param.5), kind=kOutput, calls=%fused_computation.12 | convolution fusion | flops 10774380544 | bytes 24117248 | tf_op jit(solution)/shard_map/dot_general | solution.py:28
  106.2 2.9 reduce_sum.66
  109.0 21.5 %psum.37 = bf16[1024]{0:T(1024)(128)(2,1)S(1)} all-reduce(bf16[1024]{0:T(1024)(128)(2,1)S(1)} %reduce_sum.66), channel_id=1, replica_groups=mesh['client'=8,'head'=4] {'client'}, use_global_device_ids=true, to_apply=%region_8.9 | all-reduce | flops 1024 | bytes 4096 | tf_op jit(solution)/shard_map/psum | solution.py:56
  130.5 0.6 fusion.18
  131.1 22.5 %reduce-scatter.11.cloned.1.call-done = bf16[16,1024]{1,0:T(8,128)(2,1)} async-done(((bf16[128,1024]{1,0:T(8,128)(2,1)}), bf16[16,1024]{1,0:T(8,128)(2,1)}) %reduce-scatter.11.cloned.1.call-update) | async-done | bytes 32784 | tf_op jit(solution)/shard_map/reduce_scatter | solution.py:60
  153.6 1.4 fusion.16
  155.0 70.9 %all-reduce.3.cloned.1.call-done = bf16[80,1024]{1,0:T(8,128)(2,1)} async-done(((bf16[80,1024]{1,0:T(8,128)(2,1)}), bf16[80,1024]{1,0:T(8,128)(2,1)}) %all-reduce.3.cloned.1.call-update) | async-done | bytes 163856 | tf_op jit(solution)/shard_map/psum | solution.py:55
  225.9 1.6 fusion.15
  228.8 147.9 %reduce-scatter.5.cloned.1.call-done = bf16[512,1024]{1,0:T(8,128)(2,1)} async-done(((bf16[4096,1024]{1,0:T(8,128)(2,1)}), bf16[512,1024]{1,0:T(8,128)(2,1)}) %reduce-scatter.5.cloned.1.call-update) | async-done | bytes 1048592 | tf_op jit(solution)/shard_map/reduce_scatter | solution.py:27
  376.7 2.4 fusion.12
  379.0 39.5 %all-reduce = (f32[]{:T(128)}, f32[]{:T(128)}, f32[]{:T(128)}) all-reduce(f32[]{:T(128)} %fusion.12, f32[]{:T(128)S(6)} %mul.61, f32[]{:T(128)} %fusion.16), channel_id=1, replica_groups=mesh['client'=8,'head'=4] {'client','head'}, use_global_device_ids=true, to_apply=%region_2.3 | all-reduce | flops 3 | bytes 24 | tf_op jit(solution)/shard_map/psum | solution.py:36
  419.9 0.6 convert_multiply_fusion.8
  421.2 1.7 convert_multiply_fusion.4
  422.9 1.4 convert_multiply_fusion.6
  424.3 2.8 convert_multiply_fusion.2
  (11 shorter events, 0.2 us)
Async XLA Ops:
  7.2 54.9 %reduce-scatter.9.cloned.1.call-start = ((), (), s32[]{:S(2)}) async-start(), calls=%async_computation.7 | async-start | bytes 163840 | tf_op jit(solution)/shard_map/reduce_scatter | solution.py:47
  7.2 17.6 %copy-start = (bf16[1280,4096]{1,0:T(8,128)(2,1)S(1)}, bf16[1280,4096]{1,0:T(8,128)(2,1)}, u32[]{:S(2)}) copy-start(bf16[1280,4096]{1,0:T(8,128)(2,1)} %param.4) | copy-start | bytes 31457284
  34.4 27.7 %copy-start.1 = (s32[16]{0:T(128)S(1)}, s32[16]{0:T(128)}, u32[]{:S(2)}) copy-start(s32[16]{0:T(128)} %param.7) | copy-start | bytes 196
  39.6 48.0 %reduce-scatter.7.cloned.1.call-start = ((), (), s32[]{:S(2)}) async-start(), calls=%async_computation.5 | async-start | bytes 819200 | tf_op jit(solution)/shard_map/reduce_scatter | solution.py:50
  40.3 113.3 %reduce-scatter.11.cloned.1.call-start = ((), (), s32[]{:S(2)}) async-start(), calls=%async_computation.8 | async-start | bytes 294912 | tf_op jit(solution)/shard_map/reduce_scatter | solution.py:60
  63.8 162.1 %all-reduce.3.cloned.1.call-start = ((), (), s32[]{:S(2)}) async-start(), calls=%async_computation.6 | async-start | bytes 327680 | tf_op jit(solution)/shard_map/psum | solution.py:55
  87.6 289.0 %reduce-scatter.5.cloned.1.call-start = ((), (), s32[]{:S(2)}) async-start(), calls=%async_computation.4 | async-start | bytes 9437184 | tf_op jit(solution)/shard_map/reduce_scatter | solution.py:27
Sparse Core Ops, SparseCore 0:
  39.7 22.3 reduce-scatter.8
  65.1 22.4 reduce-scatter.6
  91.5 62.0 reduce-scatter.10
  156.8 69.0 all-reduce.2
  229.3 147.2 reduce-scatter.4
where the time goes:
time: 434 us
  waiting for transfers between devices  288 us (66%)
  blocking collectives  61 us (14%)
  matrix products  37.5 us (9%)
  other arithmetic  30 us (7%)
  between operations  17.2 us (4%)
    reduce_scatter x1, waiting for transfers between devices, per_device(): lax.psum_scatter(lax.dot_general(hidden, delta_low, (((0,), (0,)), ((), (...  148 us
    psum x1, waiting for transfers between devices, per_device(): lax.psum(span_part.astype(jnp.bfloat16), 'client').astype(jnp.float32)  70.9 us
    psum x1, blocking collectives, per_device(): head_square = lax.psum(head_square, ('client', 'head'))  39.5 us
    reduce_scatter x1, waiting for transfers between devices, per_device(): lax.psum_scatter(span_whole.astype(jnp.bfloat16), 'head', scatter_dimensi...  23.8 us
    reduce_scatter x1, waiting for transfers between devices, per_device(): lax.psum_scatter(jnp.dot(selector, client_part, precision=lax.Precision.H...  22.5 us
    reduce_scatter x1, waiting for transfers between devices, per_device(): lax.psum_scatter(client_whole.astype(jnp.bfloat16), 'head', scatter_dimen...  21.7 us
    psum x1, blocking collectives, per_device(): lax.psum(bias_local.astype(jnp.bfloat16), 'client').astype(jnp.float32)  21.5 us
    dot_general x1, matrix products, per_device(): lax.dot_general(hidden, delta_low, (((0,), (0,)), ((), ())), preferred_el...  18.3 us
  transfers between devices with their start and end apart: 5, of which 5 were waited for; matrix products, arithmetic and copies ran while one was open for 6% of the time, Pallas kernels for 0%

commit v1 on v0

--- a/solution.py
+++ b/solution.py
@@ -2,6 +2,7 @@
 import jax.numpy as jnp
 from jax import lax
 from jax.sharding import PartitionSpec as P
+from jax.lax import all_gather
 
 EPSILON = 1e-06
 
@@ -52,7 +53,9 @@
         ).astype(jnp.float32),
     )
     span_raw, bias_raw = (
-        lax.psum(span_part.astype(jnp.bfloat16), "client").astype(jnp.float32),
+        jnp.sum(all_gather(span_part.astype(jnp.bfloat16), axis_name="client"), 0).astype(
+            jnp.float32
+        ),
         lax.psum(bias_local.astype(jnp.bfloat16), "client").astype(jnp.float32),
     )
     targets = lax.iota(jnp.int32, lax.axis_size("client") * clients_here)

time: 434 us -> 403 us (0.929)
  waiting for transfers between devices: 288 us -> 257 us
    psum x1 -> x0, waiting for transfers between devices: 70.9 us -> none  [per_device(): lax.psum(span_part.astype(jnp.bfloat16), 'client').astype(jnp.float32)]
    all_gather x0 -> x1, waiting for transfers between devices: none -> 41.5 us  [per_device(): all_gather(span_part.astype(jnp.bfloat16), axis_name='client')]
  transfers between devices with their start and end apart: 5 -> 5, of which waited for: 5 -> 5; matrix products, arithmetic and copies ran while one was open for 6% -> 7% of each run, Pallas kernels for 0% -> 0%
where the time goes in v1:
time: 403 us; the launch traced here: 402 us
  waiting for transfers between devices  257 us (64%)
  blocking collectives  61 us (15%)
  matrix products  37.5 us (9%)
  other arithmetic  29.8 us (7%)
  between operations  17.2 us (4%)
    reduce_scatter x1, waiting for transfers between devices, per_device(): lax.psum_scatter(lax.dot_general(hidden, delta_low, (((0,), (0,)), ((), (...  146 us
    all_gather x1, waiting for transfers between devices, per_device(): all_gather(span_part.astype(jnp.bfloat16), axis_name='client')  41.5 us
    psum x1, blocking collectives, per_device(): head_square = lax.psum(head_square, ('client', 'head'))  39.6 us
    reduce_scatter x1, waiting for transfers between devices, per_device(): lax.psum_scatter(span_whole.astype(jnp.bfloat16), 'head', scatter_dimensi...  23.8 us
    reduce_scatter x1, waiting for transfers between devices, per_device(): lax.psum_scatter(jnp.dot(selector, client_part, precision=lax.Precision.H...  22.6 us
    reduce_scatter x1, waiting for transfers between devices, per_device(): lax.psum_scatter(client_whole.astype(jnp.bfloat16), 'head', scatter_dimen...  21.7 us
    psum x1, blocking collectives, per_device(): lax.psum(bias_local.astype(jnp.bfloat16), 'client').astype(jnp.float32)  21.4 us
    dot_general x1, matrix products, per_device(): lax.dot_general(hidden, delta_low, (((0,), (0,)), ((), ())), preferred_el...  18.3 us
  transfers between devices with their start and end apart: 5, of which 5 were waited for; matrix products, arithmetic and copies ran while one was open for 7% of the time, Pallas kernels for 0%

profile of v1, /device:TPU:0, one launch (start us, length us, event | category | flops | bytes accessed | tf_op | source)
XLA Modules:
  0.0 402.5 jit_solution(3674433585175292580)
XLA Ops:
  7.2 17.6 %convolution_convert_fusion = bf16[1280,4096]{1,0:T(8,128)(2,1)} fusion(bf16[4096,1024]{1,0:T(8,128)(2,1)} %param.6, f32[1280,1024]{1,0:T(8,128)} %param.5), kind=kOutput, calls=%fused_computation.10 | convolution fusion | flops 10743971840 | bytes 24117248 | tf_op jit(solution)/shard_map/dot_general | solution.py:39
  24.8 9.6 %fusion.6 = f32[1280,4096]{1,0:T(8,128)S(1)} fusion(bf16[1280,4096]{1,0:T(8,128)(2,1)S(1)} %copy-done, bf16[1280,4096]{1,0:T(8,128)(2,1)} %convolution_convert_fusion), kind=kLoop, calls=%fused_computation.9 | loop fusion | flops 52428800 | bytes 41943040 | tf_op jit(solution)/shard_map/mul | solution.py:43
  34.4 5.2 %fusion.20 = (bf16[16,4096]{1,0:T(8,128)(2,1)}, bf16[80,4096]{1,0:T(8,128)(2,1)}) fusion(f32[16,80,4096]{2,1,0:T(8,128)S(1)} %bitcast.4), kind=kLoop, calls=%fused_computation.31 | loop fusion | flops 10092544 | bytes 21757952 | tf_op jit(solution)/shard_map/reduce_sum | solution.py:45
  39.6 0.7 reduce-scatter.7.cloned.1.call-update
  40.4 21.7 %reduce-scatter.9.cloned.1.call-done = bf16[16,1024]{1,0:T(8,128)(2,1)} async-done(((bf16[16,4096]{1,0:T(8,128)(2,1)}), bf16[16,1024]{1,0:T(8,128)(2,1)}) %reduce-scatter.9.cloned.1.call-update) | async-done | bytes 32784 | tf_op jit(solution)/shard_map/reduce_scatter | solution.py:48
  62.1 1.7 convolution_convert_fusion.1
  63.8 23.8 %reduce-scatter.7.cloned.1.call-done = bf16[80,1024]{1,0:T(8,128)(2,1)} async-done(((bf16[80,4096]{1,0:T(8,128)(2,1)}), bf16[80,1024]{1,0:T(8,128)(2,1)}) %reduce-scatter.7.cloned.1.call-update) | async-done | bytes 163856 | tf_op jit(solution)/shard_map/reduce_scatter | solution.py:51
  87.6 0.2 reduce-scatter.5.cloned.1.call-start
  87.9 18.3 %fusion.9 = bf16[4096,1024]{1,0:T(8,128)(2,1)} fusion(bf16[1280,4096]{1,0:T(8,128)(2,1)} %param.4, f32[1280,1024]{1,0:T(8,128)} %param.5), kind=kOutput, calls=%fused_computation.12 | convolution fusion | flops 10774380544 | bytes 24117248 | tf_op jit(solution)/shard_map/dot_general | solution.py:29
  106.2 2.9 reduce_sum.79
  109.0 21.4 %psum.29 = bf16[1024]{0:T(1024)(128)(2,1)S(1)} all-reduce(bf16[1024]{0:T(1024)(128)(2,1)S(1)} %reduce_sum.79), channel_id=1, replica_groups=mesh['client'=8,'head'=4] {'client'}, use_global_device_ids=true, to_apply=%region_8.9 | all-reduce | flops 1024 | bytes 4096 | tf_op jit(solution)/shard_map/psum | solution.py:59
  130.5 0.6 fusion.18
  131.1 22.6 %reduce-scatter.11.cloned.1.call-done = bf16[16,1024]{1,0:T(8,128)(2,1)} async-done(((bf16[128,1024]{1,0:T(8,128)(2,1)}), bf16[16,1024]{1,0:T(8,128)(2,1)}) %reduce-scatter.11.cloned.1.call-update) | async-done | bytes 32784 | tf_op jit(solution)/shard_map/reduce_scatter | solution.py:63
  153.6 1.4 fusion.16
  155.0 41.5 %all-gather.3.cloned.1.call-done = bf16[640,1024]{1,0:T(8,128)(2,1)} async-done(((bf16[80,1024]{1,0:T(8,128)(2,1)}), bf16[640,1024]{1,0:T(8,128)(2,1)}) %all-gather.3.cloned.1.call-update) | async-done | bytes 1310736 | tf_op jit(solution)/shard_map/all_gather | solution.py:56
  196.6 1.6 reduce_sum.77
  198.1 0.7 fusion.15
  200.1 146.3 %reduce-scatter.5.cloned.1.call-done = bf16[512,1024]{1,0:T(8,128)(2,1)} async-done(((bf16[4096,1024]{1,0:T(8,128)(2,1)}), bf16[512,1024]{1,0:T(8,128)(2,1)}) %reduce-scatter.5.cloned.1.call-update) | async-done | bytes 1048592 | tf_op jit(solution)/shard_map/reduce_scatter | solution.py:28
  346.4 2.4 fusion.12
  348.8 39.6 %all-reduce = (f32[]{:T(128)}, f32[]{:T(128)}, f32[]{:T(128)}) all-reduce(f32[]{:T(128)} %fusion.12, f32[]{:T(128)S(6)} %mul.61, f32[]{:T(128)} %fusion.16), channel_id=1, replica_groups=mesh['client'=8,'head'=4] {'client','head'}, use_global_device_ids=true, to_apply=%region_2.3 | all-reduce | flops 3 | bytes 24 | tf_op jit(solution)/shard_map/psum | solution.py:37
  389.0 0.8 convert_multiply_fusion.4
  389.8 0.6 convert_multiply_fusion.8
  391.7 1.4 convert_multiply_fusion.6
  393.1 2.8 convert_multiply_fusion.2
  (12 shorter events, 0.2 us)
Async XLA Ops:
  7.2 54.9 %reduce-scatter.9.cloned.1.call-start = ((), (), s32[]{:S(2)}) async-start(), calls=%async_computation.6 | async-start | bytes 163840 | tf_op jit(solution)/shard_map/reduce_scatter | solution.py:48
  7.2 17.6 %copy-start = (bf16[1280,4096]{1,0:T(8,128)(2,1)S(1)}, bf16[1280,4096]{1,0:T(8,128)(2,1)}, u32[]{:S(2)}) copy-start(bf16[1280,4096]{1,0:T(8,128)(2,1)} %param.4) | copy-start | bytes 31457284
  34.4 27.7 %copy-start.1 = (s32[16]{0:T(128)S(1)}, s32[16]{0:T(128)}, u32[]{:S(2)}) copy-start(s32[16]{0:T(128)} %param.7) | copy-start | bytes 196
  39.6 48.0 %reduce-scatter.7.cloned.1.call-start = ((), (), s32[]{:S(2)}) async-start(), calls=%async_computation.5 | async-start | bytes 819200 | tf_op jit(solution)/shard_map/reduce_scatter | solution.py:51
  40.3 113.3 %reduce-scatter.11.cloned.1.call-start = ((), (), s32[]{:S(2)}) async-start(), calls=%async_computation.7 | async-start | bytes 294912 | tf_op jit(solution)/shard_map/reduce_scatter | solution.py:63
  63.8 132.8 %all-gather.3.cloned.1.call-start = ((), (), s32[]{:S(2)}) async-start(), calls=%async_computation.8 | async-start | bytes 1474560 | tf_op jit(solution)/shard_map/all_gather | solution.py:56
  87.6 258.7 %reduce-scatter.5.cloned.1.call-start = ((), (), s32[]{:S(2)}) async-start(), calls=%async_computation.4 | async-start | bytes 9437184 | tf_op jit(solution)/shard_map/reduce_scatter | solution.py:28
Sparse Core Ops, SparseCore 0:
  39.7 22.3 reduce-scatter.8
  65.1 22.4 reduce-scatter.6
  91.5 62.0 reduce-scatter.10
  155.7 40.8 all-gather.2
  200.0 146.3 reduce-scatter.4
